TPU v7x, 32 devices: a whole 2x2x4 slice. The times are simulated.
32 devices in a mesh: batch: 2 (over x), row: 4 (over z), col: 4 (over y, core).
Axes of the slice: x: 2, y: 2, z: 4, core: 2. Of those that a mesh axis runs over, the one named last changes fastest.
Arguments:
- left_op: bfloat16 [14336, 7168], P(('batch', 'row'), 'col'), parts along dimension 0
- left_start: float32 [14336, 256], P(('batch', 'row', 'col')), parts along dimension 0
- right_op: bfloat16 [4096, 2048], P(('batch', 'row'), 'col'), parts along dimension 0
- right_start: float32 [4096, 256], P(('batch', 'row', 'col')), parts along dimension 0
Outputs:
- output 1: float32 [14336, 256], P(('batch', 'row', 'col')), parts along dimension 0
- output 2: float32 [512, 256], P('batch'), parts along dimension 0
- output 3: float32 [4096, 256], P(('batch', 'row', 'col')), parts along dimension 0
- output 4: float32 [512, 256], P('batch'), parts along dimension 0
There are 2 independent parts. A program takes and returns all parts, laid end to end along the dimension named above; each array names one.
All inputs are finite; a program needn't handle non-finite values.
Results may differ from a plain program's by a relative error of at most 0.001.
Values are sent between devices in bfloat16 or wider.
A program may use at most 1 GiB of HBM per device.

v0:
```python
import jax
import jax.numpy as jnp
from jax import lax
from jax.sharding import PartitionSpec as P

SWEEPS = 4
ROW_CONTRACT = (((0,), (0,)), ((), ()))


def gram_total(lhs_mat, rhs_mat, precision, grid_axes):
    local_gram = lax.dot_general(lhs_mat, rhs_mat, ROW_CONTRACT, precision=precision, preferred_element_type=jnp.float32)
    return lax.psum(local_gram, grid_axes)


def cholqr_step(y_mat, gram_mat):
    chol_low = jnp.linalg.cholesky(gram_mat)
    return lax.linalg.triangular_solve(chol_low, y_mat, left_side=False, lower=True, transpose_a=True)


def orthonormalize(y_sub, total_rows, grid_axes):
    y_half = y_sub.astype(jnp.bfloat16)
    gram_one = gram_total(y_half, y_half, None, grid_axes) / total_rows
    y_one = cholqr_step(y_sub, gram_one)
    gram_two = gram_total(y_one, y_one, lax.Precision.HIGHEST, grid_axes) / total_rows
    return cholqr_step(y_one, gram_two)


def solution(mesh):
    row_size = mesh.shape["row"]
    col_size = mesh.shape["col"]
    grid_axes = ("row", "col")
    perm_pairs = [(src_index, (src_index % row_size) * col_size + src_index // row_size) for src_index in range(row_size * col_size)]

    def apply_op(op_blk, x_sub):
        x_moved = lax.ppermute(x_sub.astype(jnp.bfloat16), grid_axes, perm_pairs)
        x_col = lax.all_gather(x_moved, "row", axis=0, tiled=True)
        partial_prod = jnp.dot(op_blk, x_col, preferred_element_type=jnp.float32)
        return lax.psum_scatter(partial_prod, "col", scatter_dimension=0, tiled=True)

    def iterate_local(op_blk, start_sub):
        total_rows = op_blk.shape[0] * row_size
        x_sub = start_sub
        for sweep_index in range(SWEEPS):
            x_sub = orthonormalize(apply_op(op_blk, x_sub), total_rows, grid_axes)
        z_sub = apply_op(op_blk, x_sub)
        rayleigh = gram_total(x_sub, z_sub, lax.Precision.HIGHEST, grid_axes) / total_rows
        return x_sub, rayleigh

    def local_program(left_op, left_start, right_op, right_start):
        left_basis, left_rayleigh = iterate_local(left_op, left_start)
        right_basis, right_rayleigh = iterate_local(right_op, right_start)
        return left_basis, left_rayleigh, right_basis, right_rayleigh

    op_spec = P(("batch", "row"), "col")
    vec_spec = P(("batch", "row", "col"), None)
    small_spec = P("batch", None)
    return jax.shard_map(local_program, mesh=mesh, in_specs=(op_spec, vec_spec, op_spec, vec_spec), out_specs=(vec_spec, small_spec, vec_spec, small_spec), check_vma=False)
```

profile of v0, /device:TPU:0, one launch (start us, length us, event | category | flops | bytes accessed | tf_op | source)
XLA Modules:
  0.0 2298.5 jit_solution(11985154395959297479)
XLA Ops:
  10.6 26.7 %all_gather.35 = bf16[512,256]{1,0:T(8,128)(2,1)S(1)} all-gather(bf16[128,256]{1,0:T(8,128)(2,1)S(1)} %collective-permute-done.5), channel_id=1, replica_groups=mesh['batch'=2,'row'=4,'col'=4] {'row'}, dimensions={0}, use_global_device_ids=true | all-gather | bytes 327680 | tf_op jit(solution)/shard_map/all_gather | solution.py:36
  66.1 27.7 %reduce-scatter.19.cloned.1.call-done = f32[448,256]{1,0:T(8,128)} async-done(((f32[1792,256]{1,0:T(8,128)}), f32[448,256]{1,0:T(8,128)}) %reduce-scatter.19.cloned.1.call-update) | async-done | bytes 458768 | tf_op jit(solution)/shard_map/reduce_scatter | solution.py:38
  96.4 93.3 %all-reduce.36.cloned.1.call-done = (f32[256,256]{0,1:T(8,128)}, f32[256,256]{0,1:T(8,128)}) async-done(((f32[256,256]{0,1:T(8,128)}, f32[256,256]{0,1:T(8,128)}), (f32[256,256]{0,1:T(8,128)}, f32[256,256]{0,1:T(8,128)})) %all-reduce.36.cloned.1.call-update) | async-done | bytes 524304 | tf_op jit(solution)/shard_map/psum | solution.py:12
  233.5 20.3 custom-call.60
  319.0 91.0 %all-reduce.34.cloned.1.call-done = (f32[256,256]{0,1:T(8,128)}, f32[256,256]{0,1:T(8,128)}) async-done(((f32[256,256]{0,1:T(8,128)}, f32[256,256]{0,1:T(8,128)}), (f32[256,256]{0,1:T(8,128)}, f32[256,256]{0,1:T(8,128)})) %all-reduce.34.cloned.1.call-update) | async-done | bytes 524304 | tf_op jit(solution)/shard_map/psum | solution.py:12
  537.5 24.2 %all_gather.36 = bf16[512,256]{0,1:T(8,128)(2,1)S(1)} all-gather(bf16[128,256]{0,1:T(8,128)(2,1)S(1)} %collective-permute-done.6), channel_id=1, replica_groups=mesh['batch'=2,'row'=4,'col'=4] {'row'}, dimensions={0}, use_global_device_ids=true | all-gather | bytes 327680 | tf_op jit(solution)/shard_map/all_gather | solution.py:36
  591.2 26.5 %reduce-scatter.31.cloned.1.call-done = f32[448,256]{1,0:T(8,128)} async-done(((f32[1792,256]{1,0:T(8,128)}), f32[448,256]{1,0:T(8,128)}) %reduce-scatter.31.cloned.1.call-update) | async-done | bytes 458768
  620.1 93.4 %all-reduce.32.cloned.1.call-done = (f32[256,256]{0,1:T(8,128)}, f32[256,256]{0,1:T(8,128)}) async-done(((f32[256,256]{0,1:T(8,128)}, f32[256,256]{0,1:T(8,128)}), (f32[256,256]{0,1:T(8,128)}, f32[256,256]{0,1:T(8,128)})) %all-reduce.32.cloned.1.call-update) | async-done | bytes 524304 | tf_op jit(solution)/shard_map/psum | solution.py:12
  756.1 20.1 custom-call.64
  843.9 91.0 %all-reduce.30.cloned.1.call-done = (f32[256,256]{0,1:T(8,128)}, f32[256,256]{0,1:T(8,128)}) async-done(((f32[256,256]{0,1:T(8,128)}, f32[256,256]{0,1:T(8,128)}), (f32[256,256]{0,1:T(8,128)}, f32[256,256]{0,1:T(8,128)})) %all-reduce.30.cloned.1.call-update) | async-done | bytes 524304 | tf_op jit(solution)/shard_map/psum | solution.py:12
  1062.4 24.2 %all_gather.37 = bf16[512,256]{0,1:T(8,128)(2,1)S(1)} all-gather(bf16[128,256]{0,1:T(8,128)(2,1)S(1)} %collective-permute-done.7), channel_id=1, replica_groups=mesh['batch'=2,'row'=4,'col'=4] {'row'}, dimensions={0}, use_global_device_ids=true | all-gather | bytes 327680 | tf_op jit(solution)/shard_map/all_gather | solution.py:36
  1116.1 26.5 %reduce-scatter.33.cloned.1.call-done = f32[448,256]{1,0:T(8,128)} async-done(((f32[1792,256]{1,0:T(8,128)}), f32[448,256]{1,0:T(8,128)}) %reduce-scatter.33.cloned.1.call-update) | async-done | bytes 458768
  1145.0 93.4 %all-reduce.28.cloned.1.call-done = (f32[256,256]{0,1:T(8,128)}, f32[256,256]{0,1:T(8,128)}) async-done(((f32[256,256]{0,1:T(8,128)}, f32[256,256]{0,1:T(8,128)}), (f32[256,256]{0,1:T(8,128)}, f32[256,256]{0,1:T(8,128)})) %all-reduce.28.cloned.1.call-update) | async-done | bytes 524304 | tf_op jit(solution)/shard_map/psum | solution.py:12
  1281.0 20.1 custom-call.68
  1368.8 91.1 %all-reduce.26.cloned.1.call-done = (f32[256,256]{0,1:T(8,128)}, f32[256,256]{0,1:T(8,128)}) async-done(((f32[256,256]{0,1:T(8,128)}, f32[256,256]{0,1:T(8,128)}), (f32[256,256]{0,1:T(8,128)}, f32[256,256]{0,1:T(8,128)})) %all-reduce.26.cloned.1.call-update) | async-done | bytes 524304 | tf_op jit(solution)/shard_map/psum | solution.py:12
  1587.4 24.2 %all_gather.38 = bf16[512,256]{0,1:T(8,128)(2,1)S(1)} all-gather(bf16[128,256]{0,1:T(8,128)(2,1)S(1)} %collective-permute-done.8), channel_id=1, replica_groups=mesh['batch'=2,'row'=4,'col'=4] {'row'}, dimensions={0}, use_global_device_ids=true | all-gather | bytes 327680 | tf_op jit(solution)/shard_map/all_gather | solution.py:36
  1641.1 26.5 %reduce-scatter.35.cloned.1.call-done = f32[448,256]{1,0:T(8,128)} async-done(((f32[1792,256]{1,0:T(8,128)}), f32[448,256]{1,0:T(8,128)}) %reduce-scatter.35.cloned.1.call-update) | async-done | bytes 458768
  1670.0 93.3 %all-reduce.24.cloned.1.call-done = (f32[256,256]{0,1:T(8,128)}, f32[256,256]{0,1:T(8,128)}) async-done(((f32[256,256]{0,1:T(8,128)}, f32[256,256]{0,1:T(8,128)}), (f32[256,256]{0,1:T(8,128)}, f32[256,256]{0,1:T(8,128)})) %all-reduce.24.cloned.1.call-update) | async-done | bytes 524304 | tf_op jit(solution)/shard_map/psum | solution.py:12
  1805.8 20.1 custom-call.72
  1869.0 19.9 custom-call.56
  1893.7 91.0 %all-reduce.22.cloned.1.call-done = (f32[256,256]{0,1:T(8,128)}, f32[256,256]{0,1:T(8,128)}) async-done(((f32[256,256]{0,1:T(8,128)}, f32[256,256]{0,1:T(8,128)}), (f32[256,256]{0,1:T(8,128)}, f32[256,256]{0,1:T(8,128)})) %all-reduce.22.cloned.1.call-update) | async-done | bytes 524304 | tf_op jit(solution)/shard_map/psum | solution.py:12
  2112.2 24.2 %all_gather.39 = bf16[512,256]{0,1:T(8,128)(2,1)S(1)} all-gather(bf16[128,256]{0,1:T(8,128)(2,1)S(1)} %collective-permute-done.9), channel_id=1, replica_groups=mesh['batch'=2,'row'=4,'col'=4] {'row'}, dimensions={0}, use_global_device_ids=true | all-gather | bytes 327680 | tf_op jit(solution)/shard_map/all_gather | solution.py:36
  2165.9 26.4 %reduce-scatter.37.cloned.1.call-done = f32[448,256]{1,0:T(8,128)} async-done(((f32[1792,256]{1,0:T(8,128)}), f32[448,256]{1,0:T(8,128)}) %reduce-scatter.37.cloned.1.call-update) | async-done | bytes 458768
  2195.9 92.3 %all-reduce.20.cloned.1.call-done = (f32[256,256]{0,1:T(8,128)}, f32[256,256]{0,1:T(8,128)}) async-done(((f32[256,256]{0,1:T(8,128)}, f32[256,256]{0,1:T(8,128)}), (f32[256,256]{0,1:T(8,128)}, f32[256,256]{0,1:T(8,128)})) %all-reduce.20.cloned.1.call-update) | async-done | bytes 524304 | tf_op jit(solution)/shard_map/psum | solution.py:12
  (569 shorter events, 1137.4 us)
Async XLA Ops:
  7.2 56.9 %reduce-scatter.21.cloned.1.call-start = ((), (), s32[]{:S(2)}) async-start(), calls=%async_computation.11 | async-start | bytes 655360 | tf_op jit(solution)/shard_map/reduce_scatter | solution.py:38
  9.9 28.5 %collective-permute-start = (bf16[448,256]{1,0:T(8,128)(2,1)S(1)}, bf16[448,256]{1,0:T(8,128)(2,1)S(1)}, u32[]{:S(2)}, u32[]{:S(2)}) collective-permute-start(bf16[448,256]{1,0:T(8,128)(2,1)S(1)} %convert_element_type.54), channel_id=1, source_target_pairs={{0,0},{1,4},{2,8},{3,12},{4,1},{5,5},{6,9},{7,13},{8,2},{9,6},{10,... | collective-permute-start | bytes 688136 | tf_op jit(solution)/shard_map/ppermute | solution.py:35
  38.4 55.4 %reduce-scatter.19.cloned.1.call-start = ((), (), s32[]{:S(2)}) async-start(), calls=%async_computation.10 | async-start | bytes 2293760 | tf_op jit(solution)/shard_map/reduce_scatter | solution.py:38
  64.0 125.7 %all-reduce.36.cloned.1.call-start = ((), (), s32[]{:S(2)}) async-start(), calls=%async_computation.28 | async-start | bytes 1048576 | tf_op jit(solution)/shard_map/psum | solution.py:12
  96.1 313.9 %all-reduce.34.cloned.1.call-start = ((), (), s32[]{:S(2)}) async-start(), calls=%async_computation.27 | async-start | bytes 1048576 | tf_op jit(solution)/shard_map/psum | solution.py:12
  318.9 270.3 %reduce-scatter.23.cloned.1.call-start = ((), (), s32[]{:S(2)}) async-start(), calls=%async_computation.12 | async-start | bytes 655360 | tf_op jit(solution)/shard_map/reduce_scatter | solution.py:38
  473.3 64.2 %collective-permute-start.6 = (bf16[128,256]{0,1:T(8,128)(2,1)S(1)}, bf16[128,256]{0,1:T(8,128)(2,1)S(1)}, u32[]{:S(2)}, u32[]{:S(2)}) collective-permute-start(bf16[128,256]{0,1:T(8,128)(2,1)S(1)} %maximum_convert_fusion.3), channel_id=1, source_target_pairs={{0,0},{1,4},{2,8},{3,12},{4,1},{5,5},{6,9},{7,13},{8,2},{9,6},{10,... | collective-permute-start | bytes 196616 | tf_op jit(solution)/shard_map/ppermute | solution.py:35
  562.9 54.8 %reduce-scatter.31.cloned.1.call-start = ((), (), s32[]{:S(2)}) async-start(), calls=%async_computation.16 | async-start | bytes 2293760
  589.2 124.4 %all-reduce.32.cloned.1.call-start = ((), (), s32[]{:S(2)}) async-start(), calls=%async_computation.26 | async-start | bytes 1048576 | tf_op jit(solution)/shard_map/psum | solution.py:12
  619.9 315.0 %all-reduce.30.cloned.1.call-start = ((), (), s32[]{:S(2)}) async-start(), calls=%async_computation.25 | async-start | bytes 1048576 | tf_op jit(solution)/shard_map/psum | solution.py:12
  843.9 270.3 %reduce-scatter.25.cloned.1.call-start = ((), (), s32[]{:S(2)}) async-start(), calls=%async_computation.13 | async-start | bytes 655360 | tf_op jit(solution)/shard_map/reduce_scatter | solution.py:38
  998.3 64.2 %collective-permute-start.7 = (bf16[128,256]{0,1:T(8,128)(2,1)S(1)}, bf16[128,256]{0,1:T(8,128)(2,1)S(1)}, u32[]{:S(2)}, u32[]{:S(2)}) collective-permute-start(bf16[128,256]{0,1:T(8,128)(2,1)S(1)} %maximum_convert_fusion.4), channel_id=1, source_target_pairs={{0,0},{1,4},{2,8},{3,12},{4,1},{5,5},{6,9},{7,13},{8,2},{9,6},{10,... | collective-permute-start | bytes 196616 | tf_op jit(solution)/shard_map/ppermute | solution.py:35
  1087.8 54.8 %reduce-scatter.33.cloned.1.call-start = ((), (), s32[]{:S(2)}) async-start(), calls=%async_computation.17 | async-start | bytes 2293760
  1114.1 124.3 %all-reduce.28.cloned.1.call-start = ((), (), s32[]{:S(2)}) async-start(), calls=%async_computation.24 | async-start | bytes 1048576 | tf_op jit(solution)/shard_map/psum | solution.py:12
  1144.8 315.1 %all-reduce.26.cloned.1.call-start = ((), (), s32[]{:S(2)}) async-start(), calls=%async_computation.23 | async-start | bytes 1048576 | tf_op jit(solution)/shard_map/psum | solution.py:12
  1368.8 270.4 %reduce-scatter.27.cloned.1.call-start = ((), (), s32[]{:S(2)}) async-start(), calls=%async_computation.14 | async-start | bytes 655360 | tf_op jit(solution)/shard_map/reduce_scatter | solution.py:38
  1523.2 64.2 %collective-permute-start.8 = (bf16[128,256]{0,1:T(8,128)(2,1)S(1)}, bf16[128,256]{0,1:T(8,128)(2,1)S(1)}, u32[]{:S(2)}, u32[]{:S(2)}) collective-permute-start(bf16[128,256]{0,1:T(8,128)(2,1)S(1)} %maximum_convert_fusion.5), channel_id=1, source_target_pairs={{0,0},{1,4},{2,8},{3,12},{4,1},{5,5},{6,9},{7,13},{8,2},{9,6},{10,... | collective-permute-start | bytes 196616 | tf_op jit(solution)/shard_map/ppermute | solution.py:35
  1612.8 54.8 %reduce-scatter.35.cloned.1.call-start = ((), (), s32[]{:S(2)}) async-start(), calls=%async_computation.18 | async-start | bytes 2293760
  1639.1 124.2 %all-reduce.24.cloned.1.call-start = ((), (), s32[]{:S(2)}) async-start(), calls=%async_computation.22 | async-start | bytes 1048576 | tf_op jit(solution)/shard_map/psum | solution.py:12
  1669.8 314.9 %all-reduce.22.cloned.1.call-start = ((), (), s32[]{:S(2)}) async-start(), calls=%async_computation.21 | async-start | bytes 1048576 | tf_op jit(solution)/shard_map/psum | solution.py:12
  1893.6 270.3 %reduce-scatter.29.cloned.1.call-start = ((), (), s32[]{:S(2)}) async-start(), calls=%async_computation.15 | async-start | bytes 655360 | tf_op jit(solution)/shard_map/reduce_scatter | solution.py:38
  2048.2 64.0 %collective-permute-start.9 = (bf16[128,256]{0,1:T(8,128)(2,1)S(1)}, bf16[128,256]{0,1:T(8,128)(2,1)S(1)}, u32[]{:S(2)}, u32[]{:S(2)}) collective-permute-start(bf16[128,256]{0,1:T(8,128)(2,1)S(1)} %fusion.218), channel_id=1, source_target_pairs={{0,0},{1,4},{2,8},{3,12},{4,1},{5,5},{6,9},{7,13},{8,2},{9,6},{10,... | collective-permute-start | bytes 196616 | tf_op jit(solution)/shard_map/ppermute | solution.py:35
  2137.5 54.8 %reduce-scatter.37.cloned.1.call-start = ((), (), s32[]{:S(2)}) async-start(), calls=%async_computation.19 | async-start | bytes 2293760
  2163.8 124.3 %all-reduce.20.cloned.1.call-start = ((), (), s32[]{:S(2)}) async-start(), calls=%async_computation.20 | async-start | bytes 1048576 | tf_op jit(solution)/shard_map/psum | solution.py:12
  (16 other events, 1449.9 us)
Sparse Core Ops, SparseCore 0:
  38.5 22.3 reduce-scatter.20
  64.1 29.6 reduce-scatter.18
  97.8 91.7 all-reduce.35
  319.0 90.9 all-reduce.33
  563.0 22.3 reduce-scatter.22
  589.3 28.3 reduce-scatter.30
  621.7 91.8 all-reduce.31
  844.0 90.8 all-reduce.29
  1088.0 22.3 reduce-scatter.24
  1114.2 28.3 reduce-scatter.32
  1146.6 91.7 all-reduce.27
  1368.9 90.9 all-reduce.25
  1612.9 22.3 reduce-scatter.26
  1639.2 28.3 reduce-scatter.34
  1671.4 91.7 all-reduce.23
  1893.7 90.8 all-reduce.21
  2137.7 22.3 reduce-scatter.28
  2164.0 28.3 reduce-scatter.36
  2196.3 91.7 all-reduce.19
where the time goes:
time: 2300 us
  waiting for transfers between devices  964 us (42%)
  other arithmetic  902 us (39%)
  blocking collectives  222 us (10%)
  matrix products  83.1 us (4%)
  local copies, waits for them, and re-layouts  79 us (3%)
  between operations  37.1 us (2%)
    psum x9, waiting for transfers between devices, gram_total(): return lax.psum(local_gram, grid_axes)  830 us
    another operation x112, other arithmetic, cholqr_step(): chol_low = jnp.linalg.cholesky(gram_mat)  553 us
    another operation x34, other arithmetic, cholqr_step(): lax.linalg.triangular_solve(chol_low, y_mat, left_side=False, lower=True,...  318 us
    all_gather x10, blocking collectives, apply_op(): x_col = lax.all_gather(x_moved, 'row', axis=0, tiled=True)  222 us
    unnamed x23, waiting for transfers between devices  106 us
    another operation x113, local copies, waits for them, and re-layouts, cholqr_step(): lax.linalg.triangular_solve(chol_low, y_mat, left_side=False, lower=True,...  63.5 us
  transfers between devices with their start and end apart: 29, of which 14 were waited for; matrix products, arithmetic and copies ran while one was open for 13% of the time, Pallas kernels for 0%

commit v1 on v0

v1 whole, which is shorter than its diff:
```python
import jax
import jax.numpy as jnp
from jax import lax
from jax.experimental import pallas as pl
from jax.experimental.pallas import tpu as pltpu
from jax.sharding import PartitionSpec as P

SWEEPS = 4
MESH = pl.DeviceIdType.MESH
HI = lax.Precision.HIGHEST
NB = 32


def dot_hi(a, b, dims):
    return lax.dot_general(a, b, (dims, ((), ())), precision=HI, preferred_element_type=jnp.float32)


def diag_block(blk_l, blk_r, lane0):
    lane = lax.broadcasted_iota(jnp.int32, (NB, 128), 1)
    row = lax.broadcasted_iota(jnp.int32, (NB, 128), 0)
    is_left = (lane // NB) % 2 == 0
    groups = NB // 8
    cols = []
    for g in range(groups):
        r0 = 8 * g
        cols.append(jnp.stack([
            jnp.where(is_left[r0:], blk_l[r0:, lane0 + k:lane0 + k + 1], blk_r[r0:, lane0 + k:lane0 + k + 1])
            for k in range(r0, r0 + 8)]))
    w = jnp.where(lane % NB == row, 1.0, 0.0)
    piv = []
    for j in range(NB):
        g0, jj = divmod(j, 8)
        r0 = 8 * g0
        u = cols[g0][0]
        p = u[jj:jj + 1]
        piv.append(p)
        if j == NB - 1:
            break
        m = jnp.where(row[r0:] > j, u * (1.0 / p), 0.0)
        if jj < 7:
            cols[g0] = cols[g0][1:] - m[None] * u[jj + 1:8][:, None, :]
        for g in range(g0 + 1, groups):
            d = 8 * (g - g0)
            cols[g] = cols[g] - m[d:][None] * u[d:d + 8][:, None, :]
        w_low = w[r0:] - m * w[j:j + 1]
        w = w_low if g0 == 0 else jnp.concatenate([w[:r0], w_low], axis=0)
    return w * lax.rsqrt(jnp.concatenate(piv, axis=0))


def chol_inverse(s, w):
    lane64 = lax.broadcasted_iota(jnp.int32, (NB, 128), 1)
    rowi = lax.broadcasted_iota(jnp.int32, (256, 256), 0)
    lanei = lax.broadcasted_iota(jnp.int32, (256, 256), 1)
    for o in range(2):
        w[o] = jnp.where(rowi == lanei, 1.0, 0.0)
    for h in range(2):
        base = 128 * h
        for b in range(4):
            r0 = base + NB * b
            rows = slice(r0, r0 + NB)
            grp = slice(base, base + 128)
            li = diag_block(s[0, rows, grp], s[1, rows, grp], NB * b)
            lhs = jnp.concatenate([jnp.where(lane64 < NB, li, 0.0), jnp.where((lane64 >= NB) & (lane64 < 2 * NB), li, 0.0)], axis=0)[:, :2 * NB]
            rhs = jnp.concatenate([jnp.concatenate([s[o, rows, base:256], w[o, rows, 0:base + 128]], axis=1) for o in range(2)], axis=0)
            pan = dot_hi(lhs, rhs, ((1,), (0,)))
            ns = 256 - base
            for o in range(2):
                po = pan[NB * o:NB * o + NB]
                s[o, rows, base:256] = po[:, :ns]
                w[o, rows, 0:base + 128] = po[:, ns:]
                if b < 3:
                    pt = po[:, 0:128].T[NB * (b + 1):]
                    upd = dot_hi(pt, po, ((1,), (0,)))
                    rest = slice(r0 + NB, base + 128)
                    s[o, rest, base:256] = s[o, rest, base:256] - upd[:, :ns]
                    w[o, rest, 0:base + 128] = w[o, rest, 0:base + 128] - upd[:, ns:]
        if h == 0:
            for o in range(2):
                pb = s[o, 0:128, 128:256]
                full = jnp.concatenate([pb, w[o, 0:128, 0:128]], axis=1)
                upd = dot_hi(pb.T, full, ((1,), (0,)))
                s[o, 128:256, 128:256] = s[o, 128:256, 128:256] - upd[:, :128]
                w[o, 128:256, 0:128] = w[o, 128:256, 0:128] - upd[:, 128:]


def remote(src, dst, send_sem, recv_sem, row, col):
    return pltpu.make_async_remote_copy(src_ref=src, dst_ref=dst, send_sem=send_sem, recv_sem=recv_sem, device_id={"row": row, "col": col}, device_id_type=MESH)


def place():
    z = lax.axis_index("row")
    c = lax.axis_index("col")
    return z, c, c // 2, c % 2


def entry_barrier():
    z, c, y, core = place()
    barrier = pltpu.get_barrier_semaphore()
    peers = []
    k = z * 2 + y
    for e in range(1, 8):
        q = (k + e) % 8
        peers.append((q // 2, (q % 2) * 2 + core))
    peers.append((z, 2 * y + 1 - core))
    peers.append((z, 2 * (1 - y) + 1 - core))
    for row, col in peers:
        pl.semaphore_signal(barrier, inc=1, device_id={"row": row, "col": col}, device_id_type=MESH)
    pl.semaphore_wait(barrier, len(peers))


def product(ops, xs, ys, bufs):
    z, c, y, core = place()
    xb, zbuf, xcol, zs, zr, cs, cr = bufs["gather"]
    dsend, drecv, ysend, yrecv, ds, dr, yss, yrs = bufs["scatter"]
    partner = 2 * y + 1 - core
    across = 2 * (1 - y) + core

    def gather_copy(o, d):
        return remote(xb[o], zbuf[o].at[d], zs.at[o, d], zr.at[o, d], (z + d) % 4, c)

    def cross_copy(o, d):
        src = xb[o] if d == 0 else zbuf[o].at[d]
        to = (z - d + 4) % 4
        return to, remote(src, xcol[o].at[c], cs.at[o, d], cr.at[o, c], z, to)

    for o in range(2):
        xb[o][...] = xs[o][...].astype(jnp.bfloat16)
    for o in range(2):
        for d in (2, 1, 3):
            gather_copy(o, d).start()
    for d in (0, 1, 3, 2):
        for o in range(2):
            if d:
                gather_copy(o, d).wait_recv()
            to, copy = cross_copy(o, d)

            @pl.when(to != c)
            def _():
                copy.start()

            @pl.when(to == c)
            def _():
                xcol[o][c] = xb[o][...] if d == 0 else zbuf[o][d]

    for o in range(2):
        for e in range(1, 4):
            frm = (c + e) % 4
            remote(xb[o], xcol[o].at[frm], cs.at[o, 0], cr.at[o, frm], z, frm).wait_recv()
        n = xs[o].shape[0]
        full = xcol[o][...].reshape(4 * n, 256)

        def part(q):
            return jnp.dot(ops[o][pl.ds(pl.multiple_of(q * n, n), n), :], full, preferred_element_type=jnp.float32)

        def d2d(i):
            return remote(dsend[o].at[i], drecv[o].at[i], ds.at[o, i], dr.at[o, i], z, partner)

        dsend[o][0] = part(2 * (1 - y) + 1 - core)
        d2d(0).start()
        mine = part(2 * (1 - y) + core)
        d2d(0).wait_recv()
        ysend[o][...] = mine + drecv[o][0]
        remote(ysend[o], yrecv[o], yss.at[o], yrs.at[o], z, across).start()
        dsend[o][1] = part(2 * y + 1 - core)
        d2d(1).start()
        mine = part(2 * y + core)
        d2d(1).wait_recv()
        ys[o][...] = mine + drecv[o][1]
    for o in (1, 0):
        hop = remote(ysend[o], yrecv[o], yss.at[o], yrs.at[o], z, across)
        hop.wait_recv()
        ys[o][...] = ys[o][...] + yrecv[o][...]
        hop.wait_send()
        for i in range(2):
            remote(dsend[o].at[i], drecv[o].at[i], ds.at[o, i], dr.at[o, i], z, partner).wait_send()
        for d in range(1, 4):
            gather_copy(o, d).wait_send()
        for d in range(4):
            to, copy = cross_copy(o, d)

            @pl.when(to != c)
            def _():
                copy.wait_send()


def all_sum(half, bufs):
    z, c, y, core = place()
    gp, r1, acc, r2, res, s1, s2, s3, s4, v1, v2, v3, v4 = bufs["sum"]
    partner = 2 * y + 1 - core
    piece = half // 8
    k = z * 2 + y

    def peer(e):
        q = (k + e) % 8
        return q, q // 2, (q % 2) * 2 + core

    one = remote(gp.at[1 - core, pl.ds(0, half)], r1.at[pl.ds(0, half)], s1, v1, z, partner)
    one.start()
    one.wait_recv()
    acc[0:half] = gp[core, 0:half] + r1[0:half]

    def spread(e):
        q, row, col = peer(e)
        return remote(acc.at[pl.ds(pl.multiple_of(q * piece, piece), piece)], r2.at[e, pl.ds(0, piece)], s2.at[e], v2.at[e], row, col)

    order = (4, 3, 5, 2, 6, 1, 7)
    for e in order:
        spread(e).start()
    mine = pl.ds(pl.multiple_of(k * piece, piece), piece)
    total = acc[mine]
    for e in range(1, 8):
        spread(e).wait_recv()
        total = total + r2[e, 0:piece]
    res[core, mine] = total

    def share(e, slot):
        q, row, col = peer(e)
        at = pl.ds(pl.multiple_of(slot * piece, piece), piece)
        return remote(res.at[core, at], res.at[core, at], s3.at[e], v3.at[e], row, col)

    for e in order:
        share(e, k).start()
    for e in range(1, 8):
        share(e, (k + 8 - e) % 8).wait_recv()
    last = remote(res.at[core, pl.ds(0, half)], res.at[core, pl.ds(0, half)], s4, v4, z, partner)
    last.start()
    got = remote(res.at[1 - core, pl.ds(0, half)], res.at[1 - core, pl.ds(0, half)], s4, v4, z, partner)
    got.wait_recv()
    one.wait_send()
    for e in range(1, 8):
        spread(e).wait_send()
        share(e, k).wait_send()
    last.wait_send()


def pack_gram(mats, precision, gp):
    for o in range(2):
        g = lax.dot_general(mats[o], mats[o], (((0,), (0,)), ((), ())), precision=precision, preferred_element_type=jnp.float32)
        gp[o, 0:128] = g[0:128, 0:128]
        gp[o, 128:256] = g[0:128, 128:256]
        gp[o, 256:384] = g[128:256, 128:256]


def body(lop, lx, rop, rx, xl_out, hl_out, xr_out, hr_out, lv, rv, xl, xr, yl, yr, s, w, *rest):
    names = iter(rest)

    def take(n):
        return [next(names) for _ in range(n)]

    xb, zbuf, xcol = take(2), take(2), take(2)
    gsems = take(4)
    dsend, drecv, ysend, yrecv = take(2), take(2), take(2), take(2)
    ssems = take(4)
    bufs = {"gather": (xb, zbuf, xcol, *gsems), "scatter": (dsend, drecv, ysend, yrecv, *ssems), "sum": take(13)}
    (lsem,) = take(1)
    loads = [pltpu.make_async_copy(lop, lv, lsem.at[0]), pltpu.make_async_copy(rop, rv, lsem.at[1])]
    for load in loads:
        load.start()
    xs, ys, ops = (xl, xr), (yl, yr), (lv, rv)
    scales = [1.0 / (16 * ref.shape[0]) for ref in xs]
    xl[...] = lx[...]
    xr[...] = rx[...]
    entry_barrier()
    for load in loads:
        load.wait()

    gp, res = bufs["sum"][0], bufs["sum"][4]

    def half_step(phase, carry):
        @pl.when(phase == 0)
        def _():
            pack_gram([r[...].astype(jnp.bfloat16) for r in ys], None, gp)

        @pl.when(phase == 1)
        def _():
            pack_gram([r[...] for r in ys], HI, gp)

        all_sum(384, bufs)
        for o in range(2):
            s[o, 0:128, 0:128] = res[o, 0:128] * scales[o]
            s[o, 0:128, 128:256] = res[o, 128:256] * scales[o]
            s[o, 128:256, 128:256] = res[o, 256:384] * scales[o]
        chol_inverse(s, w)
        for o in range(2):
            ys[o][...] = dot_hi(ys[o][...], w[o], ((1,), (1,)))
        return carry

    def sweep(i, carry):
        product(ops, xs, ys, bufs)
        lax.fori_loop(0, 2, half_step, 0)
        for o in range(2):
            xs[o][...] = ys[o][...]
        return carry

    lax.fori_loop(0, SWEEPS, sweep, 0)
    product(ops, xs, ys, bufs)
    for o in range(2):
        h = dot_hi(xs[o][...], ys[o][...], ((0,), (0,)))
        gp[o, 0:256] = h[:, 0:128]
        gp[o, 256:512] = h[:, 128:256]
    all_sum(512, bufs)
    for o, out in enumerate((hl_out, hr_out)):
        out[:, 0:128] = res[o, 0:256] * scales[o]
        out[:, 128:256] = res[o, 256:512] * scales[o]
    xl_out[...] = xl[...]
    xr_out[...] = xr[...]


def solution(mesh):
    f32, bf16 = jnp.float32, jnp.bfloat16

    def local_program(left_op, left_start, right_op, right_start):
        nl, nr = left_start.shape[0], right_start.shape[0]
        vm = pl.BlockSpec(memory_space=pltpu.VMEM)
        hbm = pl.BlockSpec(memory_space=pl.ANY)
        dma = pltpu.SemaphoreType.DMA

        def pair(shape, dtype):
            return [pltpu.VMEM(shape(nl), dtype), pltpu.VMEM(shape(nr), dtype)]

        scratch = [pltpu.VMEM(left_op.shape, bf16), pltpu.VMEM(right_op.shape, bf16)]
        scratch += pair(lambda n: (n, 256), f32) + pair(lambda n: (n, 256), f32)
        scratch += [pltpu.VMEM((2, 256, 256), f32), pltpu.VMEM((2, 256, 256), f32)]
        scratch += pair(lambda n: (n, 256), bf16) + pair(lambda n: (4, n, 256), bf16) + pair(lambda n: (4, n, 256), bf16)
        scratch += [dma((2, 4)), dma((2, 4)), dma((2, 4)), dma((2, 4))]
        scratch += pair(lambda n: (2, n, 256), f32) + pair(lambda n: (2, n, 256), f32)
        scratch += pair(lambda n: (n, 256), f32) + pair(lambda n: (n, 256), f32)
        scratch += [dma((2, 2)), dma((2, 2)), dma((2,)), dma((2,))]
        scratch += [pltpu.VMEM((2, 512, 128), f32), pltpu.VMEM((512, 128), f32), pltpu.VMEM((512, 128), f32), pltpu.VMEM((8, 64, 128), f32), pltpu.VMEM((2, 512, 128), f32)]
        scratch += [dma, dma((8,)), dma((8,)), dma, dma, dma((8,)), dma((8,)), dma]
        scratch += [dma((2,))]
        small = jax.ShapeDtypeStruct((256, 256), f32)
        xl, hl, xr, hr = pl.pallas_call(
            body,
            out_shape=(jax.ShapeDtypeStruct((nl, 256), f32), small, jax.ShapeDtypeStruct((nr, 256), f32), small),
            in_specs=[hbm, vm, hbm, vm],
            out_specs=(vm, vm, vm, vm),
            scratch_shapes=scratch,
            compiler_params=pltpu.CompilerParams(collective_id=0, has_side_effects=True, vmem_limit_bytes=60 * 1024 * 1024),
        )(left_op, left_start, right_op, right_start)
        return xl, hl, xr, hr

    op_spec = P(("batch", "row"), "col")
    vec_spec = P(("batch", "row", "col"), None)
    small_spec = P("batch", None)
    return jax.shard_map(local_program, mesh=mesh, in_specs=(op_spec, vec_spec, op_spec, vec_spec), out_specs=(vec_spec, small_spec, vec_spec, small_spec), check_vma=False)
```

time: 2300 us -> 513 us (0.22)
  waiting for transfers between devices: 964 us -> 0 us
  other arithmetic: 902 us -> 0 us
  Pallas kernels: 0 us -> 505 us
  blocking collectives: 222 us -> 0 us
  matrix products: 83.1 us -> 0 us
  local copies, waits for them, and re-layouts: 79 us -> 6.72 us
  between operations: 37.1 us -> 0.64 us
    another operation x146 -> x0, other arithmetic: 871 us -> none  [the longest x112 553 us: cholqr_step(): chol_low = jnp.linalg.cholesky(gram_mat)]
    psum x9 -> x0, waiting for transfers between devices: 830 us -> none  [gram_total(): return lax.psum(local_gram, grid_axes)]
    pallas_call x0 -> x1, Pallas kernels: none -> 505 us  [local_program(): pl.pallas_call(body, out_shape=(jax.ShapeDtypeStruct((nl, 256), f32), sma...]
    all_gather x10 -> x0, blocking collectives: 222 us -> none  [apply_op(): x_col = lax.all_gather(x_moved, 'row', axis=0, tiled=True)]
    unnamed x23 -> x0, waiting for transfers between devices: 106 us -> none
    another operation x145 -> x0, local copies, waits for them, and re-layouts: 63.9 us -> none  [the longest x113 63.5 us: cholqr_step(): lax.linalg.triangular_solve(chol_low, y_mat, left_side=False, lower=True,...]
    dot_general x28 -> x0, matrix products: 59.4 us -> none  [the longest x10 30.6 us: apply_op(): partial_prod = jnp.dot(op_blk, x_col, preferred_element_type=jnp.float32)]
    div x33 -> x0, other arithmetic: 28.8 us -> none  [the longest x15 11.1 us: cholqr_step(): chol_low = jnp.linalg.cholesky(gram_mat)]
  transfers between devices with their start and end apart: 29 -> 0, of which waited for: 14 -> 0; matrix products, arithmetic and copies ran while one was open for 13% -> 0% of each run, Pallas kernels for 0% -> 0%
where the time goes in v1:
time: 513 us; the launch traced here: 512 us
  Pallas kernels  505 us (98%)
  local copies, waits for them, and re-layouts  6.72 us (1%)
    pallas_call x1, Pallas kernels, local_program(): pl.pallas_call(body, out_shape=(jax.ShapeDtypeStruct((nl, 256), f32), sma...  505 us

profile of v1, /device:TPU:0, one launch (start us, length us, event | category | flops | bytes accessed | tf_op | source)
XLA Modules:
  0.0 512.5 jit_solution(11129255601136622351)
XLA Ops:
  0.6 505.1 %shard_map.75 = (f32[448,256]{1,0:T(8,128)}, f32[256,256]{1,0:T(8,128)}, f32[128,256]{1,0:T(8,128)}, f32[256,256]{1,0:T(8,128)}) custom-call(bf16[1792,1792]{1,0:T(8,128)(2,1)} %lop.1, f32[448,256]{1,0:T(8,128)} %lx.1, bf16[512,512]{1,0:T(8,128)(2,1)} %rop.1, f32[128,256]{1,0:T(8,128)} %rx.1), custom_call_target="tpu_custom_call" | custom-call | tf_op jit(solution)/shard_map/pallas_call | solution.py:333
  505.7 1.8 copy.12
  507.5 1.7 copy.13
  509.2 1.6 copy.14
  510.8 1.7 copy.15

commit v2 on v1

--- a/solution.py
+++ b/solution.py
@@ -111,74 +111,123 @@
 def product(ops, xs, ys, bufs):
     z, c, y, core = place()
     xb, zbuf, xcol, zs, zr, cs, cr = bufs["gather"]
-    dsend, drecv, ysend, yrecv, ds, dr, yss, yrs = bufs["scatter"]
+    dsend, drecv, ysend, yrecv, ds, dr_sem, yss, yrs = bufs["scatter"]
     partner = 2 * y + 1 - core
     across = 2 * (1 - y) + core
-
-    def gather_copy(o, d):
-        return remote(xb[o], zbuf[o].at[d], zs.at[o, d], zr.at[o, d], (z + d) % 4, c)
-
-    def cross_copy(o, d):
-        src = xb[o] if d == 0 else zbuf[o].at[d]
-        to = (z - d + 4) % 4
-        return to, remote(src, xcol[o].at[c], cs.at[o, d], cr.at[o, c], z, to)
-
-    for o in range(2):
-        xb[o][...] = xs[o][...].astype(jnp.bfloat16)
-    for o in range(2):
-        for d in (2, 1, 3):
-            gather_copy(o, d).start()
-    for d in (0, 1, 3, 2):
-        for o in range(2):
-            if d:
-                gather_copy(o, d).wait_recv()
-            to, copy = cross_copy(o, d)
-
-            @pl.when(to != c)
+    units = ((0, 0, 128), (0, 128, 256), (1, 0, 256))
+
+    def has(way, h):
+        return z >= h if way == 0 else z + h <= 3
+
+    def onward(way, h):
+        return (z >= h) & (z < 3) if way == 0 else (z + h <= 3) & (z > 0)
+
+    def hop(u, way, h):
+        src = xb[u] if h == 0 else zbuf[u].at[3 * way + h - 1]
+        at = 3 * way + h
+        row = (z + 1) % 4 if way == 0 else (z + 3) % 4
+        return remote(src, zbuf[u].at[at], zs.at[u, at], zr.at[u, at], row, c)
+
+    def cross(u, slot):
+        src = xb[u] if slot == 6 else zbuf[u].at[slot]
+        way, h = (0, 0) if slot == 6 else (slot // 3, slot % 3 + 1)
+        to = (z + 4 - h) % 4 if way == 0 else (z + h) % 4
+        return src, to, remote(src, xcol[u].at[c], cs.at[u, slot], cr.at[u, c], z, to)
+
+    def start_cross(u, slot):
+        src, to, copy = cross(u, slot)
+
+        @pl.when(to != c)
+        def _():
+            copy.start()
+
+        @pl.when(to == c)
+        def _():
+            xcol[u][c] = src[...]
+
+    def own(u):
+        o, c0, c1 = units[u]
+        xb[u][...] = xs[o][:, c0:c1].astype(jnp.bfloat16)
+        for way in range(2):
+            @pl.when(onward(way, 0))
             def _():
-                copy.start()
-
-            @pl.when(to == c)
+                hop(u, way, 0).start()
+        start_cross(u, 6)
+
+    def arrive(u, h):
+        for way in range(2):
+            slot = 3 * way + h - 1
+
+            @pl.when(has(way, h))
             def _():
-                xcol[o][c] = xb[o][...] if d == 0 else zbuf[o][d]
-
-    for o in range(2):
+                hop(u, way, h - 1).wait_recv()
+                if h < 3:
+                    @pl.when(onward(way, h))
+                    def _():
+                        hop(u, way, h).start()
+                start_cross(u, slot)
+
+    def d2d(u, i):
+        return remote(dsend[u].at[i], drecv[u].at[i], ds.at[u, i], dr_sem.at[u, i], z, partner)
+
+    def yhop(u):
+        return remote(ysend[u], yrecv[u], yss.at[u], yrs.at[u], z, across)
+
+    def compute(u):
+        o, c0, c1 = units[u]
         for e in range(1, 4):
             frm = (c + e) % 4
-            remote(xb[o], xcol[o].at[frm], cs.at[o, 0], cr.at[o, frm], z, frm).wait_recv()
+            remote(xb[u], xcol[u].at[frm], cs.at[u, 6], cr.at[u, frm], z, frm).wait_recv()
         n = xs[o].shape[0]
-        full = xcol[o][...].reshape(4 * n, 256)
+        full = xcol[u][...].reshape(4 * n, c1 - c0)
 
         def part(q):
             return jnp.dot(ops[o][pl.ds(pl.multiple_of(q * n, n), n), :], full, preferred_element_type=jnp.float32)
 
-        def d2d(i):
-            return remote(dsend[o].at[i], drecv[o].at[i], ds.at[o, i], dr.at[o, i], z, partner)
-
-        dsend[o][0] = part(2 * (1 - y) + 1 - core)
-        d2d(0).start()
-        mine = part(2 * (1 - y) + core)
-        d2d(0).wait_recv()
-        ysend[o][...] = mine + drecv[o][0]
-        remote(ysend[o], yrecv[o], yss.at[o], yrs.at[o], z, across).start()
-        dsend[o][1] = part(2 * y + 1 - core)
-        d2d(1).start()
-        mine = part(2 * y + core)
-        d2d(1).wait_recv()
-        ys[o][...] = mine + drecv[o][1]
-    for o in (1, 0):
-        hop = remote(ysend[o], yrecv[o], yss.at[o], yrs.at[o], z, across)
-        hop.wait_recv()
-        ys[o][...] = ys[o][...] + yrecv[o][...]
-        hop.wait_send()
+        dsend[u][0] = part(2 * (1 - y) + 1 - core)
+        d2d(u, 0).start()
+        far = part(2 * (1 - y) + core)
+        dsend[u][1] = part(2 * y + 1 - core)
+        d2d(u, 1).start()
+        d2d(u, 0).wait_recv()
+        ysend[u][...] = far + drecv[u][0]
+        yhop(u).start()
+        near = part(2 * y + core)
+        d2d(u, 1).wait_recv()
+        ys[o][:, c0:c1] = near + drecv[u][1]
+
+    own(0)
+    own(1)
+    arrive(0, 1)
+    own(2)
+    arrive(1, 1)
+    arrive(0, 2)
+    arrive(2, 1)
+    arrive(1, 2)
+    arrive(0, 3)
+    arrive(2, 2)
+    arrive(1, 3)
+    compute(0)
+    arrive(2, 3)
+    compute(1)
+    compute(2)
+    for u, (o, c0, c1) in enumerate(units):
+        yhop(u).wait_recv()
+        ys[o][:, c0:c1] = ys[o][:, c0:c1] + yrecv[u][...]
+    for u in range(3):
+        yhop(u).wait_send()
         for i in range(2):
-            remote(dsend[o].at[i], drecv[o].at[i], ds.at[o, i], dr.at[o, i], z, partner).wait_send()
-        for d in range(1, 4):
-            gather_copy(o, d).wait_send()
-        for d in range(4):
-            to, copy = cross_copy(o, d)
-
-            @pl.when(to != c)
+            d2d(u, i).wait_send()
+        for way in range(2):
+            for h in range(3):
+                @pl.when(onward(way, h))
+                def _():
+                    hop(u, way, h).wait_send()
+        for slot in range(7):
+            _, to, copy = cross(u, slot)
+            here = True if slot == 6 else has(slot // 3, slot % 3 + 1)
+
+            @pl.when((to != c) & here)
             def _():
                 copy.wait_send()
 
@@ -247,9 +296,9 @@
     def take(n):
         return [next(names) for _ in range(n)]
 
-    xb, zbuf, xcol = take(2), take(2), take(2)
+    xb, zbuf, xcol = take(3), take(3), take(3)
     gsems = take(4)
-    dsend, drecv, ysend, yrecv = take(2), take(2), take(2), take(2)
+    dsend, drecv, ysend, yrecv = take(3), take(3), take(3), take(3)
     ssems = take(4)
     bufs = {"gather": (xb, zbuf, xcol, *gsems), "scatter": (dsend, drecv, ysend, yrecv, *ssems), "sum": take(13)}
     (lsem,) = take(1)
@@ -318,14 +367,18 @@
         def pair(shape, dtype):
             return [pltpu.VMEM(shape(nl), dtype), pltpu.VMEM(shape(nr), dtype)]
 
+        def units(lead, dtype):
+            return [pltpu.VMEM(lead + tail, dtype) for tail in ((nl, 128), (nl, 128), (nr, 256))]
+
         scratch = [pltpu.VMEM(left_op.shape, bf16), pltpu.VMEM(right_op.shape, bf16)]
         scratch += pair(lambda n: (n, 256), f32) + pair(lambda n: (n, 256), f32)
         scratch += [pltpu.VMEM((2, 256, 256), f32), pltpu.VMEM((2, 256, 256), f32)]
-        scratch += pair(lambda n: (n, 256), bf16) + pair(lambda n: (4, n, 256), bf16) + pair(lambda n: (4, n, 256), bf16)
-        scratch += [dma((2, 4)), dma((2, 4)), dma((2, 4)), dma((2, 4))]
-        scratch += pair(lambda n: (2, n, 256), f32) + pair(lambda n: (2, n, 256), f32)
-        scratch += pair(lambda n: (n, 256), f32) + pair(lambda n: (n, 256), f32)
-        scratch += [dma((2, 2)), dma((2, 2)), dma((2,)), dma((2,))]
+        for lead in ((), (6,), (4,)):
+            scratch += units(lead, bf16)
+        scratch += [dma((3, 6)), dma((3, 6)), dma((3, 7)), dma((3, 4))]
+        for lead in ((2,), (2,), (), ()):
+            scratch += units(lead, f32)
+        scratch += [dma((3, 2)), dma((3, 2)), dma((3,)), dma((3,))]
         scratch += [pltpu.VMEM((2, 512, 128), f32), pltpu.VMEM((512, 128), f32), pltpu.VMEM((512, 128), f32), pltpu.VMEM((8, 64, 128), f32), pltpu.VMEM((2, 512, 128), f32)]
         scratch += [dma, dma((8,)), dma((8,)), dma, dma, dma((8,)), dma((8,)), dma]
         scratch += [dma((2,))]

time: 513 us -> 446 us (0.87)
  Pallas kernels: 505 us -> 438 us
    pallas_call x1, Pallas kernels: 505 us -> 438 us  [local_program(): pl.pallas_call(body, out_shape=(jax.ShapeDtypeStruct((nl, 256), f32), sma...]
where the time goes in v2:
time: 446 us; the launch traced here: 445 us
  Pallas kernels  438 us (98%)
  local copies, waits for them, and re-layouts  6.72 us (2%)
    pallas_call x1, Pallas kernels, local_program(): pl.pallas_call(body, out_shape=(jax.ShapeDtypeStruct((nl, 256), f32), sma...  438 us

profile of v2, /device:TPU:0, one launch (start us, length us, event | category | flops | bytes accessed | tf_op | source)
XLA Modules:
  0.0 445.3 jit_solution(9248742711606998511)
XLA Ops:
  0.6 437.9 %shard_map.75 = (f32[448,256]{1,0:T(8,128)}, f32[256,256]{1,0:T(8,128)}, f32[128,256]{1,0:T(8,128)}, f32[256,256]{1,0:T(8,128)}) custom-call(bf16[1792,1792]{1,0:T(8,128)(2,1)} %lop.1, f32[448,256]{1,0:T(8,128)} %lx.1, bf16[512,512]{1,0:T(8,128)(2,1)} %rop.1, f32[128,256]{1,0:T(8,128)} %rx.1), custom_call_target="tpu_custom_call" | custom-call | tf_op jit(solution)/shard_map/pallas_call | solution.py:386
  438.5 1.8 copy.12
  440.3 1.7 copy.13
  442.0 1.6 copy.14
  443.6 1.7 copy.15

commit v3 on v2

--- a/solution.py
+++ b/solution.py
@@ -110,105 +110,146 @@
 
 def product(ops, xs, ys, bufs):
     z, c, y, core = place()
-    xb, zbuf, xcol, zs, zr, cs, cr = bufs["gather"]
+    xb, obuf, xcol, ss, rr, orr = bufs["gather"]
     dsend, drecv, ysend, yrecv, ds, dr_sem, yss, yrs = bufs["scatter"]
     partner = 2 * y + 1 - core
     across = 2 * (1 - y) + core
-    units = ((0, 0, 128), (0, 128, 256), (1, 0, 256))
-
-    def has(way, h):
-        return z >= h if way == 0 else z + h <= 3
-
-    def onward(way, h):
-        return (z >= h) & (z < 3) if way == 0 else (z + h <= 3) & (z > 0)
-
-    def hop(u, way, h):
-        src = xb[u] if h == 0 else zbuf[u].at[3 * way + h - 1]
-        at = 3 * way + h
-        row = (z + 1) % 4 if way == 0 else (z + 3) % 4
-        return remote(src, zbuf[u].at[at], zs.at[u, at], zr.at[u, at], row, c)
-
-    def cross(u, slot):
-        src = xb[u] if slot == 6 else zbuf[u].at[slot]
-        way, h = (0, 0) if slot == 6 else (slot // 3, slot % 3 + 1)
-        to = (z + 4 - h) % 4 if way == 0 else (z + h) % 4
-        return src, to, remote(src, xcol[u].at[c], cs.at[u, slot], cr.at[u, c], z, to)
-
-    def start_cross(u, slot):
-        src, to, copy = cross(u, slot)
-
-        @pl.when(to != c)
-        def _():
-            copy.start()
-
-        @pl.when(to == c)
-        def _():
-            xcol[u][c] = src[...]
+    units = ((1, 0, 256), (0, 0, 128), (0, 128, 256))
+    t = z + y * (3 - 2 * z)
+    kind = core + y * (1 - 2 * core)
+    home = t == kind
+    step = 1 - 2 * y
+    ahead, back = (z + step + 4) % 4, (z - step + 4) % 4
+    slots = (c, partner, 2 * (1 - y), 2 * (1 - y) + 1)
+    inner = jnp.where(t == 3, 0, 1)
+    target = 2 * (1 - y) + jnp.where(y == 1, inner, 1 - inner)
+
+    def goes_ahead(i):
+        return ((kind == 0) & (t < 3)) | ((kind == 1) & (t >= 1) & (t < 3) & (i < 2))
+
+    goes_back = (kind == 1) & (t == 1)
+
+    def pass_on(u, i, way):
+        at = xcol[u].at[slots[i]]
+        return remote(at, at, ss.at[u, 4 * way + i], rr.at[u, slots[i]], back if way else ahead, c)
+
+    def start_passes(u, i):
+        @pl.when(goes_ahead(i))
+        def _():
+            pass_on(u, i, 0).start()
+
+        @pl.when(goes_back)
+        def _():
+            pass_on(u, i, 1).start()
+
+    def to_partner(u):
+        return remote(xb[u], xcol[u].at[c], ss.at[u, 8], rr.at[u, c], z, partner)
+
+    gives = (t == 1 - kind) & (t < 2)
+
+    def cross(u, src):
+        return remote(src, xcol[u].at[c], ss.at[u, 9], rr.at[u, c], z, target)
+
+    def ride(u, src):
+        return remote(src, obuf[u], ss.at[u, 10], orr.at[u], back, c)
+
+    def arrived(u, i):
+        remote(xb[u], xcol[u].at[slots[i]], ss.at[u, 9], rr.at[u, slots[i]], z, target).wait_recv()
 
     def own(u):
         o, c0, c1 = units[u]
         xb[u][...] = xs[o][:, c0:c1].astype(jnp.bfloat16)
-        for way in range(2):
-            @pl.when(onward(way, 0))
-            def _():
-                hop(u, way, 0).start()
-        start_cross(u, 6)
-
-    def arrive(u, h):
-        for way in range(2):
-            slot = 3 * way + h - 1
-
-            @pl.when(has(way, h))
-            def _():
-                hop(u, way, h - 1).wait_recv()
-                if h < 3:
-                    @pl.when(onward(way, h))
-                    def _():
-                        hop(u, way, h).start()
-                start_cross(u, slot)
+
+        @pl.when(t >= 2)
+        def _():
+            cross(u, xb[u]).start()
+
+        @pl.when(t == 2)
+        def _():
+            ride(u, xb[u]).start()
+
+        @pl.when(gives)
+        def _():
+            to_partner(u).start()
+
+        @pl.when(home)
+        def _():
+            xcol[u][c] = xb[u][...]
+            start_passes(u, 0)
+
+    def stage(u, i, who=True):
+        @pl.when((goes_ahead(i) | goes_back) & who)
+        def _():
+            if i == 0:
+                @pl.when(jnp.logical_not(home))
+                def _():
+                    arrived(u, 0)
+                    start_passes(u, 0)
+            else:
+                arrived(u, i)
+                start_passes(u, i)
+
+    def transit(u, at):
+        @pl.when(t == at)
+        def _():
+            ride(u, xb[u]).wait_recv()
+            if at == 1:
+                ride(u, obuf[u]).start()
+            cross(u, obuf[u]).start()
 
     def d2d(u, i):
-        return remote(dsend[u].at[i], drecv[u].at[i], ds.at[u, i], dr_sem.at[u, i], z, partner)
+        return remote(dsend[u].at[i, 1 - core], drecv[u].at[i], ds.at[u, i], dr_sem.at[u, i], z, partner)
 
     def yhop(u):
         return remote(ysend[u], yrecv[u], yss.at[u], yrs.at[u], z, across)
 
     def compute(u):
         o, c0, c1 = units[u]
-        for e in range(1, 4):
-            frm = (c + e) % 4
-            remote(xb[u], xcol[u].at[frm], cs.at[u, 6], cr.at[u, frm], z, frm).wait_recv()
+        for i in range(4):
+            @pl.when(jnp.logical_not(goes_ahead(i) | goes_back))
+            def _():
+                arrived(u, i)
+
         n = xs[o].shape[0]
         full = xcol[u][...].reshape(4 * n, c1 - c0)
 
-        def part(q):
-            return jnp.dot(ops[o][pl.ds(pl.multiple_of(q * n, n), n), :], full, preferred_element_type=jnp.float32)
-
-        dsend[u][0] = part(2 * (1 - y) + 1 - core)
-        d2d(u, 0).start()
-        far = part(2 * (1 - y) + core)
-        dsend[u][1] = part(2 * y + 1 - core)
-        d2d(u, 1).start()
+        def half_rows(i, of):
+            rows = ops[o][pl.ds(pl.multiple_of(of * 2 * n, 2 * n), 2 * n), :]
+            dsend[u][i] = jnp.dot(rows, full, preferred_element_type=jnp.float32).reshape(2, n, c1 - c0)
+            d2d(u, i).start()
+
+        half_rows(0, 1 - y)
+        half_rows(1, y)
         d2d(u, 0).wait_recv()
-        ysend[u][...] = far + drecv[u][0]
+        ysend[u][...] = dsend[u][0, core] + drecv[u][0]
         yhop(u).start()
-        near = part(2 * y + core)
         d2d(u, 1).wait_recv()
-        ys[o][:, c0:c1] = near + drecv[u][1]
+        ys[o][:, c0:c1] = dsend[u][1, core] + drecv[u][1]
 
     own(0)
     own(1)
-    arrive(0, 1)
+    stage(0, 0)
+    stage(0, 1)
     own(2)
-    arrive(1, 1)
-    arrive(0, 2)
-    arrive(2, 1)
-    arrive(1, 2)
-    arrive(0, 3)
-    arrive(2, 2)
-    arrive(1, 3)
+    transit(0, 1)
+    stage(0, 2)
+    stage(0, 3)
+    stage(1, 0)
+    stage(1, 1)
+    transit(1, 1)
+    stage(1, 2)
+    stage(1, 3)
+    for i in range(4):
+        stage(2, i, t == 0)
+    transit(0, 0)
+    transit(1, 0)
     compute(0)
-    arrive(2, 3)
+    stage(2, 0, t > 0)
+    stage(2, 1, t > 0)
+    transit(2, 1)
+    stage(2, 2, t > 0)
+    stage(2, 3, t > 0)
+    transit(2, 0)
     compute(1)
     compute(2)
     for u, (o, c0, c1) in enumerate(units):
@@ -218,18 +259,24 @@
         yhop(u).wait_send()
         for i in range(2):
             d2d(u, i).wait_send()
-        for way in range(2):
-            for h in range(3):
-                @pl.when(onward(way, h))
-                def _():
-                    hop(u, way, h).wait_send()
-        for slot in range(7):
-            _, to, copy = cross(u, slot)
-            here = True if slot == 6 else has(slot // 3, slot % 3 + 1)
-
-            @pl.when((to != c) & here)
+        for i in range(4):
+            @pl.when(goes_ahead(i))
             def _():
-                copy.wait_send()
+                pass_on(u, i, 0).wait_send()
+
+            @pl.when(goes_back)
+            def _():
+                pass_on(u, i, 1).wait_send()
+
+        @pl.when(gives)
+        def _():
+            to_partner(u).wait_send()
+
+        cross(u, xb[u]).wait_send()
+
+        @pl.when((t == 1) | (t == 2))
+        def _():
+            ride(u, xb[u]).wait_send()
 
 
 def all_sum(half, bufs):
@@ -296,11 +343,11 @@
     def take(n):
         return [next(names) for _ in range(n)]
 
-    xb, zbuf, xcol = take(3), take(3), take(3)
-    gsems = take(4)
+    xb, obuf, xcol = take(3), take(3), take(3)
+    gsems = take(3)
     dsend, drecv, ysend, yrecv = take(3), take(3), take(3), take(3)
     ssems = take(4)
-    bufs = {"gather": (xb, zbuf, xcol, *gsems), "scatter": (dsend, drecv, ysend, yrecv, *ssems), "sum": take(13)}
+    bufs = {"gather": (xb, obuf, xcol, *gsems), "scatter": (dsend, drecv, ysend, yrecv, *ssems), "sum": take(13)}
     (lsem,) = take(1)
     loads = [pltpu.make_async_copy(lop, lv, lsem.at[0]), pltpu.make_async_copy(rop, rv, lsem.at[1])]
     for load in loads:
@@ -368,15 +415,15 @@
             return [pltpu.VMEM(shape(nl), dtype), pltpu.VMEM(shape(nr), dtype)]
 
         def units(lead, dtype):
-            return [pltpu.VMEM(lead + tail, dtype) for tail in ((nl, 128), (nl, 128), (nr, 256))]
+            return [pltpu.VMEM(lead + tail, dtype) for tail in ((nr, 256), (nl, 128), (nl, 128))]
 
         scratch = [pltpu.VMEM(left_op.shape, bf16), pltpu.VMEM(right_op.shape, bf16)]
         scratch += pair(lambda n: (n, 256), f32) + pair(lambda n: (n, 256), f32)
         scratch += [pltpu.VMEM((2, 256, 256), f32), pltpu.VMEM((2, 256, 256), f32)]
-        for lead in ((), (6,), (4,)):
+        for lead in ((), (), (4,)):
             scratch += units(lead, bf16)
-        scratch += [dma((3, 6)), dma((3, 6)), dma((3, 7)), dma((3, 4))]
-        for lead in ((2,), (2,), (), ()):
+        scratch += [dma((3, 11)), dma((3, 4)), dma((3,))]
+        for lead in ((2, 2), (2,), (), ()):
             scratch += units(lead, f32)
         scratch += [dma((3, 2)), dma((3, 2)), dma((3,)), dma((3,))]
         scratch += [pltpu.VMEM((2, 512, 128), f32), pltpu.VMEM((512, 128), f32), pltpu.VMEM((512, 128), f32), pltpu.VMEM((8, 64, 128), f32), pltpu.VMEM((2, 512, 128), f32)]

time: 446 us -> 429 us (0.962)
  Pallas kernels: 438 us -> 421 us
    pallas_call x1, Pallas kernels: 438 us -> 421 us  [local_program(): pl.pallas_call(body, out_shape=(jax.ShapeDtypeStruct((nl, 256), f32), sma...]
where the time goes in v3:
time: 429 us
  Pallas kernels  421 us (98%)
  local copies, waits for them, and re-layouts  6.72 us (2%)
    pallas_call x1, Pallas kernels, local_program(): pl.pallas_call(body, out_shape=(jax.ShapeDtypeStruct((nl, 256), f32), sma...  421 us

profile of v3, /device:TPU:0, one launch (start us, length us, event | category | flops | bytes accessed | tf_op | source)
XLA Modules:
  0.0 428.6 jit_solution(1032299955253607554)
XLA Ops:
  0.6 421.2 %shard_map.75 = (f32[448,256]{1,0:T(8,128)}, f32[256,256]{1,0:T(8,128)}, f32[128,256]{1,0:T(8,128)}, f32[256,256]{1,0:T(8,128)}) custom-call(bf16[1792,1792]{1,0:T(8,128)(2,1)} %lop.1, f32[448,256]{1,0:T(8,128)} %lx.1, bf16[512,512]{1,0:T(8,128)(2,1)} %rop.1, f32[128,256]{1,0:T(8,128)} %rx.1), custom_call_target="tpu_custom_call" | custom-call | tf_op jit(solution)/shard_map/pallas_call | solution.py:433
  421.9 1.8 copy.12
  423.7 1.7 copy.13
  425.4 1.6 copy.14
  426.9 1.7 copy.15

commit v4 on v3

--- a/solution.py
+++ b/solution.py
@@ -15,17 +15,15 @@
     return lax.dot_general(a, b, (dims, ((), ())), precision=HI, preferred_element_type=jnp.float32)
 
 
-def diag_block(blk_l, blk_r, lane0):
+def diag_block(blk, lane0):
     lane = lax.broadcasted_iota(jnp.int32, (NB, 128), 1)
     row = lax.broadcasted_iota(jnp.int32, (NB, 128), 0)
-    is_left = (lane // NB) % 2 == 0
     groups = NB // 8
     cols = []
     for g in range(groups):
         r0 = 8 * g
         cols.append(jnp.stack([
-            jnp.where(is_left[r0:], blk_l[r0:, lane0 + k:lane0 + k + 1], blk_r[r0:, lane0 + k:lane0 + k + 1])
-            for k in range(r0, r0 + 8)]))
+            jnp.broadcast_to(blk[r0:, lane0 + k:lane0 + k + 1], (NB - r0, 128)) for k in range(r0, r0 + 8)]))
     w = jnp.where(lane % NB == row, 1.0, 0.0)
     piv = []
     for j in range(NB):
@@ -48,39 +46,29 @@
 
 
 def chol_inverse(s, w):
-    lane64 = lax.broadcasted_iota(jnp.int32, (NB, 128), 1)
     rowi = lax.broadcasted_iota(jnp.int32, (256, 256), 0)
     lanei = lax.broadcasted_iota(jnp.int32, (256, 256), 1)
-    for o in range(2):
-        w[o] = jnp.where(rowi == lanei, 1.0, 0.0)
+    w[...] = jnp.where(rowi == lanei, 1.0, 0.0)
     for h in range(2):
         base = 128 * h
         for b in range(4):
             r0 = base + NB * b
             rows = slice(r0, r0 + NB)
-            grp = slice(base, base + 128)
-            li = diag_block(s[0, rows, grp], s[1, rows, grp], NB * b)
-            lhs = jnp.concatenate([jnp.where(lane64 < NB, li, 0.0), jnp.where((lane64 >= NB) & (lane64 < 2 * NB), li, 0.0)], axis=0)[:, :2 * NB]
-            rhs = jnp.concatenate([jnp.concatenate([s[o, rows, base:256], w[o, rows, 0:base + 128]], axis=1) for o in range(2)], axis=0)
-            pan = dot_hi(lhs, rhs, ((1,), (0,)))
+            li = diag_block(s[rows, base:base + 128], NB * b)
+            pan = dot_hi(li[:, :NB], jnp.concatenate([s[rows, base:256], w[rows, 0:base + 128]], axis=1), ((1,), (0,)))
             ns = 256 - base
-            for o in range(2):
-                po = pan[NB * o:NB * o + NB]
-                s[o, rows, base:256] = po[:, :ns]
-                w[o, rows, 0:base + 128] = po[:, ns:]
-                if b < 3:
-                    pt = po[:, 0:128].T[NB * (b + 1):]
-                    upd = dot_hi(pt, po, ((1,), (0,)))
-                    rest = slice(r0 + NB, base + 128)
-                    s[o, rest, base:256] = s[o, rest, base:256] - upd[:, :ns]
-                    w[o, rest, 0:base + 128] = w[o, rest, 0:base + 128] - upd[:, ns:]
+            s[rows, base:256] = pan[:, :ns]
+            w[rows, 0:base + 128] = pan[:, ns:]
+            if b < 3:
+                upd = dot_hi(pan[:, 0:128].T[NB * (b + 1):], pan, ((1,), (0,)))
+                rest = slice(r0 + NB, base + 128)
+                s[rest, base:256] = s[rest, base:256] - upd[:, :ns]
+                w[rest, 0:base + 128] = w[rest, 0:base + 128] - upd[:, ns:]
         if h == 0:
-            for o in range(2):
-                pb = s[o, 0:128, 128:256]
-                full = jnp.concatenate([pb, w[o, 0:128, 0:128]], axis=1)
-                upd = dot_hi(pb.T, full, ((1,), (0,)))
-                s[o, 128:256, 128:256] = s[o, 128:256, 128:256] - upd[:, :128]
-                w[o, 128:256, 0:128] = w[o, 128:256, 0:128] - upd[:, 128:]
+            pb = s[0:128, 128:256]
+            upd = dot_hi(pb.T, jnp.concatenate([pb, w[0:128, 0:128]], axis=1), ((1,), (0,)))
+            s[128:256, 128:256] = s[128:256, 128:256] - upd[:, :128]
+            w[128:256, 0:128] = w[128:256, 0:128] - upd[:, 128:]
 
 
 def remote(src, dst, send_sem, recv_sem, row, col):
@@ -211,10 +199,9 @@
                 arrived(u, i)
 
         n = xs[o].shape[0]
-        full = xcol[u][...].reshape(4 * n, c1 - c0)
-
         def half_rows(i, of):
             rows = ops[o][pl.ds(pl.multiple_of(of * 2 * n, 2 * n), 2 * n), :]
+            full = xcol[u][...].reshape(4 * n, c1 - c0)
             dsend[u][i] = jnp.dot(rows, full, preferred_element_type=jnp.float32).reshape(2, n, c1 - c0)
             d2d(u, i).start()
 
@@ -279,7 +266,7 @@
             ride(u, xb[u]).wait_send()
 
 
-def all_sum(half, bufs):
+def all_sum(half, bufs, both):
     z, c, y, core = place()
     gp, r1, acc, r2, res, s1, s2, s3, s4, v1, v2, v3, v4 = bufs["sum"]
     partner = 2 * y + 1 - core
@@ -319,14 +306,15 @@
     for e in range(1, 8):
         share(e, (k + 8 - e) % 8).wait_recv()
     last = remote(res.at[core, pl.ds(0, half)], res.at[core, pl.ds(0, half)], s4, v4, z, partner)
-    last.start()
-    got = remote(res.at[1 - core, pl.ds(0, half)], res.at[1 - core, pl.ds(0, half)], s4, v4, z, partner)
-    got.wait_recv()
+    if both:
+        last.start()
+        remote(res.at[1 - core, pl.ds(0, half)], res.at[1 - core, pl.ds(0, half)], s4, v4, z, partner).wait_recv()
     one.wait_send()
     for e in range(1, 8):
         spread(e).wait_send()
         share(e, k).wait_send()
-    last.wait_send()
+    if both:
+        last.wait_send()
 
 
 def pack_gram(mats, precision, gp):
@@ -337,7 +325,7 @@
         gp[o, 256:384] = g[128:256, 128:256]
 
 
-def body(lop, lx, rop, rx, xl_out, hl_out, xr_out, hr_out, lv, rv, xl, xr, yl, yr, s, w, *rest):
+def body(lop, lx, rop, rx, xl_out, hl_out, xr_out, hr_out, lv, rv, xl, xr, yl, yr, s, w, other, wsems, *rest):
     names = iter(rest)
 
     def take(n):
@@ -361,6 +349,7 @@
         load.wait()
 
     gp, res = bufs["sum"][0], bufs["sum"][4]
+    z, c, y, core = place()
 
     def half_step(phase, carry):
         @pl.when(phase == 0)
@@ -371,14 +360,18 @@
         def _():
             pack_gram([r[...] for r in ys], HI, gp)
 
-        all_sum(384, bufs)
+        all_sum(384, bufs, False)
+        scale = jnp.where(core == 0, scales[0], scales[1])
+        s[0:128, 0:128] = res[core, 0:128] * scale
+        s[0:128, 128:256] = res[core, 128:256] * scale
+        s[128:256, 128:256] = res[core, 256:384] * scale
+        chol_inverse(s, w)
+        swap = remote(w, other, wsems.at[0], wsems.at[1], z, 2 * y + 1 - core)
+        swap.start()
+        swap.wait_recv()
         for o in range(2):
-            s[o, 0:128, 0:128] = res[o, 0:128] * scales[o]
-            s[o, 0:128, 128:256] = res[o, 128:256] * scales[o]
-            s[o, 128:256, 128:256] = res[o, 256:384] * scales[o]
-        chol_inverse(s, w)
-        for o in range(2):
-            ys[o][...] = dot_hi(ys[o][...], w[o], ((1,), (1,)))
+            ys[o][...] = dot_hi(ys[o][...], jnp.where(core == o, w[...], other[...]), ((1,), (1,)))
+        swap.wait_send()
         return carry
 
     def sweep(i, carry):
@@ -394,7 +387,7 @@
         h = dot_hi(xs[o][...], ys[o][...], ((0,), (0,)))
         gp[o, 0:256] = h[:, 0:128]
         gp[o, 256:512] = h[:, 128:256]
-    all_sum(512, bufs)
+    all_sum(512, bufs, True)
     for o, out in enumerate((hl_out, hr_out)):
         out[:, 0:128] = res[o, 0:256] * scales[o]
         out[:, 128:256] = res[o, 256:512] * scales[o]
@@ -419,7 +412,7 @@
 
         scratch = [pltpu.VMEM(left_op.shape, bf16), pltpu.VMEM(right_op.shape, bf16)]
         scratch += pair(lambda n: (n, 256), f32) + pair(lambda n: (n, 256), f32)
-        scratch += [pltpu.VMEM((2, 256, 256), f32), pltpu.VMEM((2, 256, 256), f32)]
+        scratch += [pltpu.VMEM((256, 256), f32)] * 3 + [dma((2,))]
         for lead in ((), (), (4,)):
             scratch += units(lead, bf16)
         scratch += [dma((3, 11)), dma((3, 4)), dma((3,))]

time: 429 us -> 419 us (0.977)
  Pallas kernels: 421 us -> 412 us
    pallas_call x1, Pallas kernels: 421 us -> 412 us  [local_program(): pl.pallas_call(body, out_shape=(jax.ShapeDtypeStruct((nl, 256), f32), sma...]
where the time goes in v4:
time: 419 us
  Pallas kernels  412 us (98%)
  local copies, waits for them, and re-layouts  6.72 us (2%)
    pallas_call x1, Pallas kernels, local_program(): pl.pallas_call(body, out_shape=(jax.ShapeDtypeStruct((nl, 256), f32), sma...  412 us

profile of v4, /device:TPU:0, one launch (start us, length us, event | category | flops | bytes accessed | tf_op | source)
XLA Modules:
  0.0 418.9 jit_solution(491500398893807091)
XLA Ops:
  0.6 411.5 %shard_map.75 = (f32[448,256]{1,0:T(8,128)}, f32[256,256]{1,0:T(8,128)}, f32[128,256]{1,0:T(8,128)}, f32[256,256]{1,0:T(8,128)}) custom-call(bf16[1792,1792]{1,0:T(8,128)(2,1)} %lop.1, f32[448,256]{1,0:T(8,128)} %lx.1, bf16[512,512]{1,0:T(8,128)(2,1)} %rop.1, f32[128,256]{1,0:T(8,128)} %rx.1), custom_call_target="tpu_custom_call" | custom-call | tf_op jit(solution)/shard_map/pallas_call | solution.py:426
  412.2 1.8 copy.12
  414.0 1.7 copy.13
  415.6 1.6 copy.14
  417.2 1.7 copy.15

commit v5 on v4

--- a/solution.py
+++ b/solution.py
@@ -266,9 +266,9 @@
             ride(u, xb[u]).wait_send()
 
 
-def all_sum(half, bufs, both):
+def all_sum(half, bufs, gram):
     z, c, y, core = place()
-    gp, r1, acc, r2, res, s1, s2, s3, s4, v1, v2, v3, v4 = bufs["sum"]
+    gp, r1, acc, r2, res, diag, s1, s2, s3, s4, s5, v1, v2, v3, v4, v5 = bufs["sum"]
     partner = 2 * y + 1 - core
     piece = half // 8
     k = z * 2 + y
@@ -277,24 +277,41 @@
         q = (k + e) % 8
         return q, q // 2, (q % 2) * 2 + core
 
-    one = remote(gp.at[1 - core, pl.ds(0, half)], r1.at[pl.ds(0, half)], s1, v1, z, partner)
+    rows = half + 8 if gram else half
+    one = remote(gp.at[1 - core, pl.ds(0, rows)], r1.at[pl.ds(0, rows)], s1, v1, z, partner)
     one.start()
     one.wait_recv()
-    acc[0:half] = gp[core, 0:half] + r1[0:half]
+    acc[0:rows] = gp[core, 0:rows] + r1[0:rows]
 
     def spread(e):
         q, row, col = peer(e)
         return remote(acc.at[pl.ds(pl.multiple_of(q * piece, piece), piece)], r2.at[e, pl.ds(0, piece)], s2.at[e], v2.at[e], row, col)
 
+    def spread_diag(e):
+        q, row, col = peer(e)
+        return remote(acc.at[pl.ds(half, 8)], diag.at[k], s5.at[e], v5.at[e], row, col)
+
     order = (4, 3, 5, 2, 6, 1, 7)
     for e in order:
         spread(e).start()
+        if gram:
+            spread_diag(e).start()
+    if gram:
+        diag[k] = acc[half:half + 8]
     mine = pl.ds(pl.multiple_of(k * piece, piece), piece)
     total = acc[mine]
     for e in range(1, 8):
         spread(e).wait_recv()
         total = total + r2[e, 0:piece]
     res[core, mine] = total
+    if gram:
+        for e in range(1, 8):
+            frm = (k + 8 - e) % 8
+            remote(acc.at[pl.ds(half, 8)], diag.at[frm], s5.at[e], v5.at[e], z, partner).wait_recv()
+        line = diag[0]
+        for q in range(1, 8):
+            line = line + diag[q]
+        res[core, half:half + 8] = line
 
     def share(e, slot):
         q, row, col = peer(e)
@@ -306,23 +323,33 @@
     for e in range(1, 8):
         share(e, (k + 8 - e) % 8).wait_recv()
     last = remote(res.at[core, pl.ds(0, half)], res.at[core, pl.ds(0, half)], s4, v4, z, partner)
-    if both:
+    if not gram:
         last.start()
         remote(res.at[1 - core, pl.ds(0, half)], res.at[1 - core, pl.ds(0, half)], s4, v4, z, partner).wait_recv()
     one.wait_send()
     for e in range(1, 8):
         spread(e).wait_send()
         share(e, k).wait_send()
-    if both:
+        if gram:
+            spread_diag(e).wait_send()
+    if not gram:
         last.wait_send()
 
 
+def triangle():
+    row = lax.broadcasted_iota(jnp.int32, (128, 128), 0)
+    lane = lax.broadcasted_iota(jnp.int32, (128, 128), 1)
+    return row <= lane, row == lane
+
+
 def pack_gram(mats, precision, gp):
+    above, on = triangle()
     for o in range(2):
         g = lax.dot_general(mats[o], mats[o], (((0,), (0,)), ((), ())), precision=precision, preferred_element_type=jnp.float32)
-        gp[o, 0:128] = g[0:128, 0:128]
+        low = g[128:256, 128:256]
+        gp[o, 0:128] = jnp.where(above, g[0:128, 0:128], low)
         gp[o, 128:256] = g[0:128, 128:256]
-        gp[o, 256:384] = g[128:256, 128:256]
+        gp[o, 256:264] = jnp.broadcast_to(jnp.sum(jnp.where(on, low, 0.0), axis=0, keepdims=True), (8, 128))
 
 
 def body(lop, lx, rop, rx, xl_out, hl_out, xr_out, hr_out, lv, rv, xl, xr, yl, yr, s, w, other, wsems, *rest):
@@ -335,7 +362,7 @@
     gsems = take(3)
     dsend, drecv, ysend, yrecv = take(3), take(3), take(3), take(3)
     ssems = take(4)
-    bufs = {"gather": (xb, obuf, xcol, *gsems), "scatter": (dsend, drecv, ysend, yrecv, *ssems), "sum": take(13)}
+    bufs = {"gather": (xb, obuf, xcol, *gsems), "scatter": (dsend, drecv, ysend, yrecv, *ssems), "sum": take(16)}
     (lsem,) = take(1)
     loads = [pltpu.make_async_copy(lop, lv, lsem.at[0]), pltpu.make_async_copy(rop, rv, lsem.at[1])]
     for load in loads:
@@ -360,11 +387,14 @@
         def _():
             pack_gram([r[...] for r in ys], HI, gp)
 
-        all_sum(384, bufs, False)
+        all_sum(256, bufs, True)
         scale = jnp.where(core == 0, scales[0], scales[1])
-        s[0:128, 0:128] = res[core, 0:128] * scale
+        above, on = triangle()
+        tile = res[core, 0:128] * scale
+        flip = tile.T
+        s[0:128, 0:128] = jnp.where(above, tile, flip)
         s[0:128, 128:256] = res[core, 128:256] * scale
-        s[128:256, 128:256] = res[core, 256:384] * scale
+        s[128:256, 128:256] = jnp.where(on, res[core, 256:257] * scale, jnp.where(above, flip, tile))
         chol_inverse(s, w)
         swap = remote(w, other, wsems.at[0], wsems.at[1], z, 2 * y + 1 - core)
         swap.start()
@@ -387,7 +417,7 @@
         h = dot_hi(xs[o][...], ys[o][...], ((0,), (0,)))
         gp[o, 0:256] = h[:, 0:128]
         gp[o, 256:512] = h[:, 128:256]
-    all_sum(512, bufs, True)
+    all_sum(512, bufs, False)
     for o, out in enumerate((hl_out, hr_out)):
         out[:, 0:128] = res[o, 0:256] * scales[o]
         out[:, 128:256] = res[o, 256:512] * scales[o]
@@ -419,8 +449,8 @@
         for lead in ((2, 2), (2,), (), ()):
             scratch += units(lead, f32)
         scratch += [dma((3, 2)), dma((3, 2)), dma((3,)), dma((3,))]
-        scratch += [pltpu.VMEM((2, 512, 128), f32), pltpu.VMEM((512, 128), f32), pltpu.VMEM((512, 128), f32), pltpu.VMEM((8, 64, 128), f32), pltpu.VMEM((2, 512, 128), f32)]
-        scratch += [dma, dma((8,)), dma((8,)), dma, dma, dma((8,)), dma((8,)), dma]
+        scratch += [pltpu.VMEM((2, 512, 128), f32), pltpu.VMEM((512, 128), f32), pltpu.VMEM((512, 128), f32), pltpu.VMEM((8, 64, 128), f32), pltpu.VMEM((2, 512, 128), f32), pltpu.VMEM((8, 8, 128), f32)]
+        scratch += [dma, dma((8,)), dma((8,)), dma, dma((8,))] * 2
         scratch += [dma((2,))]
         small = jax.ShapeDtypeStruct((256, 256), f32)
         xl, hl, xr, hr = pl.pallas_call(

time: 419 us -> 404 us (0.964)
  Pallas kernels: 412 us -> 397 us
    pallas_call x1, Pallas kernels: 412 us -> 397 us  [local_program(): pl.pallas_call(body, out_shape=(jax.ShapeDtypeStruct((nl, 256), f32), sma...]
where the time goes in v5:
time: 404 us
  Pallas kernels  397 us (98%)
  local copies, waits for them, and re-layouts  6.72 us (2%)
    pallas_call x1, Pallas kernels, local_program(): pl.pallas_call(body, out_shape=(jax.ShapeDtypeStruct((nl, 256), f32), sma...  397 us

profile of v5, /device:TPU:0, one launch (start us, length us, event | category | flops | bytes accessed | tf_op | source)
XLA Modules:
  0.0 404.0 jit_solution(16854297953602097743)
XLA Ops:
  0.6 396.7 %shard_map.75 = (f32[448,256]{1,0:T(8,128)}, f32[256,256]{1,0:T(8,128)}, f32[128,256]{1,0:T(8,128)}, f32[256,256]{1,0:T(8,128)}) custom-call(bf16[1792,1792]{1,0:T(8,128)(2,1)} %lop.1, f32[448,256]{1,0:T(8,128)} %lx.1, bf16[512,512]{1,0:T(8,128)(2,1)} %rop.1, f32[128,256]{1,0:T(8,128)} %rx.1), custom_call_target="tpu_custom_call" | custom-call | tf_op jit(solution)/shard_map/pallas_call | solution.py:456
  397.3 1.8 copy.12
  399.1 1.7 copy.13
  400.8 1.6 copy.14
  402.4 1.7 copy.15

commit v6 on v5

--- a/solution.py
+++ b/solution.py
@@ -199,19 +199,30 @@
                 arrived(u, i)
 
         n = xs[o].shape[0]
+        def quarter(q):
+            rows = ops[o][pl.ds(pl.multiple_of(q * n, n), n), :]
+            return jnp.dot(rows, xcol[u][...].reshape(4 * n, c1 - c0), preferred_element_type=jnp.float32)
+
         def half_rows(i, of):
             rows = ops[o][pl.ds(pl.multiple_of(of * 2 * n, 2 * n), 2 * n), :]
             full = xcol[u][...].reshape(4 * n, c1 - c0)
             dsend[u][i] = jnp.dot(rows, full, preferred_element_type=jnp.float32).reshape(2, n, c1 - c0)
             d2d(u, i).start()
 
-        half_rows(0, 1 - y)
-        half_rows(1, y)
-        d2d(u, 0).wait_recv()
-        ysend[u][...] = dsend[u][0, core] + drecv[u][0]
-        yhop(u).start()
-        d2d(u, 1).wait_recv()
-        ys[o][:, c0:c1] = dsend[u][1, core] + drecv[u][1]
+        if u < 2:
+            half_rows(0, 1 - y)
+            half_rows(1, y)
+            d2d(u, 0).wait_recv()
+            ysend[u][...] = dsend[u][0, core] + drecv[u][0]
+            yhop(u).start()
+        else:
+            dsend[u][0, 1 - core] = quarter(2 * (1 - y) + 1 - core)
+            d2d(u, 0).start()
+            far = quarter(2 * (1 - y) + core)
+            d2d(u, 0).wait_recv()
+            ysend[u][...] = far + drecv[u][0]
+            yhop(u).start()
+            half_rows(1, y)
 
     own(0)
     own(1)
@@ -240,8 +251,9 @@
     compute(1)
     compute(2)
     for u, (o, c0, c1) in enumerate(units):
+        d2d(u, 1).wait_recv()
         yhop(u).wait_recv()
-        ys[o][:, c0:c1] = ys[o][:, c0:c1] + yrecv[u][...]
+        ys[o][:, c0:c1] = dsend[u][1, core] + drecv[u][1] + yrecv[u][...]
     for u in range(3):
         yhop(u).wait_send()
         for i in range(2):

time: 404 us -> 402 us (level)
  no operation moved by 1% of the time
where the time goes in v6:
time: 402 us
  Pallas kernels  395 us (98%)
  local copies, waits for them, and re-layouts  6.72 us (2%)
    pallas_call x1, Pallas kernels, local_program(): pl.pallas_call(body, out_shape=(jax.ShapeDtypeStruct((nl, 256), f32), sma...  395 us

profile of v6, /device:TPU:0, one launch (start us, length us, event | category | flops | bytes accessed | tf_op | source)
XLA Modules:
  0.0 402.0 jit_solution(14490391975536752400)
XLA Ops:
  0.6 394.7 %shard_map.75 = (f32[448,256]{1,0:T(8,128)}, f32[256,256]{1,0:T(8,128)}, f32[128,256]{1,0:T(8,128)}, f32[256,256]{1,0:T(8,128)}) custom-call(bf16[1792,1792]{1,0:T(8,128)(2,1)} %lop.1, f32[448,256]{1,0:T(8,128)} %lx.1, bf16[512,512]{1,0:T(8,128)(2,1)} %rop.1, f32[128,256]{1,0:T(8,128)} %rx.1), custom_call_target="tpu_custom_call" | custom-call | tf_op jit(solution)/shard_map/pallas_call | solution.py:468
  395.3 1.8 copy.12
  397.1 1.7 copy.13
  398.8 1.6 copy.14
  400.3 1.7 copy.15
